TPU v7x, 32 devices: a whole 2x2x4 slice. The times are simulated.
32 devices in a mesh: row: 4 (over z), col: 8 (over y, x, core).
Axes of the slice: x: 2, y: 2, z: 4, core: 2. Of those that a mesh axis runs over, the one named last changes fastest.
Arguments:
- points_rhs: bfloat16 [262144, 16], P(('row', 'col')), may hold values from -6 to 6
- leaf_basis: bfloat16 [1024, 256, 64], P(('row', 'col')), may hold values from -0.375 to 0.375
- near_src: int32 [1024, 2], P(('row', 'col')), may hold values from -1 to 1023, as said below
- near_blocks: bfloat16 [1024, 2, 256, 256], P(('row', 'col')), may hold values from -0.25 to 0.25
- transfer_first: bfloat16 [1024, 64, 64], P(('row', 'col')), may hold values from -0.5 to 0.5
- transfer_second: bfloat16 [512, 64, 64], P(('row', 'col')), may hold values from -0.5 to 0.5
- transfer_third: bfloat16 [256, 64, 64], P(('row', 'col')), may hold values from -0.5 to 0.5
- far_zero: int32 [1024, 8], P(('row', 'col')), may hold values from -1 to 1023, as said below
- far_one: int32 [512, 8], P(('row', 'col')), may hold values from -1 to 511, as said below
- far_two: int32 [256, 8], P(('row', 'col')), may hold values from -1 to 255, as said below
- far_three: int32 [128, 8], P(('row', 'col')), may hold values from -1 to 127, as said below
- couple_zero: bfloat16 [1024, 8, 64, 64], P(('row', 'col')), may hold values from -0.25 to 0.25
- couple_one: bfloat16 [512, 8, 64, 64], P(('row', 'col')), may hold values from -0.25 to 0.25
- couple_two: bfloat16 [256, 8, 64, 64], P(('row', 'col')), may hold values from -0.25 to 0.25
- couple_three: bfloat16 [128, 8, 64, 64], P(('row', 'col')), may hold values from -0.25 to 0.25
Outputs:
- product: bfloat16 [262144, 16], P(('row', 'col'))
Inputs may be any that keep to these rules, and one draw needn't show every extreme that they name: `near_src`: each entry is -1 or a leaf whose index differs from its row's by at most 2; -1 only where that leaf would lie outside the grid. `far_zero`: each row has 7 or 8 live entries, first in the row; a live entry of leaf i lies in the same aligned block of 256 leaves as i. `far_one`: each row has 7 or 8 live entries, first in the row; a live entry of cluster i lies in the same aligned block of 128 clusters as i. `far_two`: each row has 7 or 8 live entries, first in the row; a live entry of cluster i lies in the same aligned block of 64 clusters as i. `far_three`: each row has 7 or 8 live entries, first in the row; live entries may name any cluster of the level.
All inputs are finite; a program needn't handle non-finite values.
Results may differ from a plain program's by a relative error of at most 0.0044.
Values may be sent and summed in bfloat16 or wider, within the bound.
No kernel may reach another device: no remote copies, remote signals or barrier semaphores. Data moves between devices by JAX's collectives and lax.ppermute only.
A program may use at most 128 MiB of HBM per device.

v0:
```python
import jax
import jax.numpy as jnp
from jax import lax
from jax.sharding import PartitionSpec as P

LEAF = 256
RANK = 64
NRHS = 16
TOP_LEVEL = lax.Precision.HIGHEST


def padded_2(cells, sides, width):
    for axis, dim in sides:
        count = lax.axis_size(axis)
        ends = count - 1
        head = lax.slice_in_dim(cells, 0, width, axis=dim)
        tail = lax.slice_in_dim(cells, cells.shape[dim] - width, cells.shape[dim], axis=dim)
        cells = jnp.concatenate(
            [
                lax.ppermute(tail, axis, [(i, (i + 1) % count) for i in range(ends)]),
                cells,
                lax.ppermute(head, axis, [((i + 1) % count, i) for i in range(ends)]),
            ],
            axis=dim,
        )
    return cells


def gather_active(table, local_ids, sources):
    is_live = sources >= 0
    selected_rows = jnp.take(table, jnp.clip(local_ids, 0, table.shape[0] - 1), axis=0)
    return jnp.where(is_live[:, :, None, None], selected_rows, jnp.zeros_like(selected_rows))


def couple_level(table, group_start, sources, coupling_block):
    selected_rows = gather_active(table, sources - group_start, sources)
    return jnp.einsum(
        "enyd,endc->eyc", coupling_block, selected_rows, preferred_element_type=jnp.float32
    )


def collect_group(skeleton):
    return lax.all_gather(skeleton, "col", axis=0, tiled=True)


def shards(
    points_rhs,
    leaf_basis,
    near_src,
    near_blocks,
    transfer_first,
    transfer_second,
    transfer_third,
    far_zero,
    far_one,
    far_two,
    far_three,
    couple_zero,
    couple_one,
    couple_two,
    couple_three,
):
    leaf_count = leaf_basis.shape[0]
    leaf_x = points_rhs.reshape(leaf_count, LEAF, NRHS)
    padded = padded_2(points_rhs.reshape(leaf_count, LEAF * NRHS), ((("row", "col"), 0),), 2)
    padded = padded.reshape(leaf_count + 4, LEAF, NRHS)
    skel_zero = jnp.einsum(
        "lpa,lpr->lar", leaf_basis, leaf_x, preferred_element_type=jnp.float32
    ).astype(jnp.bfloat16)
    skeletons = [skel_zero]
    transfers = [transfer_first, transfer_second, transfer_third]
    for transfer in transfers:
        child_skel = skeletons[-1]
        lifted = jnp.einsum(
            "cab,car->cbr", transfer, child_skel, preferred_element_type=jnp.float32
        )
        lifted = lifted.reshape(lifted.shape[0] // 2, 2, RANK, NRHS).sum(axis=1)
        skeletons.append(lifted.astype(jnp.bfloat16))
    tables = [collect_group(skeletons[level_index]) for level_index in range(3)]
    coarse_group = lax.all_gather(skeletons[3], "col", axis=0, tiled=True)
    coarse_table = lax.all_gather(coarse_group, "row", axis=0, tiled=True)
    row_index = lax.axis_index("row")
    lists = [far_zero, far_one, far_two]
    coupling_blocks = [couple_zero, couple_one, couple_two]
    coupled_field = []
    for level_index in range(3):
        group_start = row_index * tables[level_index].shape[0]
        coupled_field.append(
            couple_level(
                tables[level_index], group_start, lists[level_index], coupling_blocks[level_index]
            )
        )
    coupled_field.append(couple_level(coarse_table, 0, far_three, couple_three))
    downward_field = coupled_field[3]
    for level_index in (3, 2, 1):
        spread = jnp.repeat(downward_field, 2, axis=0)
        downward_field = coupled_field[level_index - 1] + jnp.einsum(
            "cab,cbr->car",
            transfers[level_index - 1].astype(jnp.float32),
            spread,
            precision=TOP_LEVEL,
        )
    far_out = jnp.einsum(
        "lpa,lar->lpr", leaf_basis.astype(jnp.float32), downward_field, precision=TOP_LEVEL
    )
    first_leaf = lax.axis_index(("row", "col")) * leaf_count
    near_picked = gather_active(padded, near_src - first_leaf + 2, near_src)
    near_out = jnp.einsum(
        "iknm,ikmr->inr", near_blocks, near_picked, preferred_element_type=jnp.float32
    )
    return (far_out + near_out).reshape(leaf_count * LEAF, NRHS).astype(jnp.bfloat16)


def solution(mesh):
    return jax.shard_map(
        shards,
        mesh=mesh,
        in_specs=(
            P(("row", "col"), None),
            P(("row", "col"), None, None),
            P(("row", "col"), None),
            P(("row", "col"), None, None, None),
            P(("row", "col"), None, None),
            P(("row", "col"), None, None),
            P(("row", "col"), None, None),
            P(("row", "col"), None),
            P(("row", "col"), None),
            P(("row", "col"), None),
            P(("row", "col"), None),
            P(("row", "col"), None, None, None),
            P(("row", "col"), None, None, None),
            P(("row", "col"), None, None, None),
            P(("row", "col"), None, None, None),
        ),
        out_specs=P(("row", "col"), None),
        check_vma=False,
    )
```

profile of v0, /device:TPU:0, one launch (start us, length us, event | category | flops | bytes accessed | tf_op | source)
XLA Modules:
  0.0 106.1 jit_solution(7011895499649475544)
XLA Ops:
  0.0 0.9 fusion.44
  1.0 0.8 slice.13
  1.8 3.0 %collective-permute-start = (bf16[2,4096]{1,0:T(2,128)(2,1)}, bf16[2,4096]{1,0:T(2,128)(2,1)}, u32[]{:S(2)}, u32[]{:S(2)}) collective-permute-start(bf16[2,4096]{1,0:T(2,128)(2,1)} %slice.13), channel_id=1, source_target_pairs={{0,1},{1,2},{2,3},{3,4},{4,5},{5,6},{6,7},{7,8},{8,9},{9,10},{10,1... | collective-permute-start | bytes 49160 | tf_op jit(solution)/shard_map/ppermute | solution.py:20
  4.9 0.8 slice.15
  5.7 1.3 %collective-permute-start.1 = (bf16[2,4096]{1,0:T(2,128)(2,1)}, bf16[2,4096]{1,0:T(2,128)(2,1)}, u32[]{:S(2)}, u32[]{:S(2)}) collective-permute-start(bf16[2,4096]{1,0:T(2,128)(2,1)} %slice.15), channel_id=1, source_target_pairs={{1,0},{2,1},{3,2},{4,3},{5,4},{6,5},{7,6},{8,7},{9,8},{10,9},{11,1... | collective-permute-start | bytes 49160 | tf_op jit(solution)/shard_map/ppermute | solution.py:22
  7.0 0.7 compare_select_fusion.3
  7.7 1.3 %broadcast_compare_fusion.3 = (pred[4,8]{1,0:T(4,128)(4,1)}, pred[4,8]{1,0:T(4,128)(4,1)}) fusion(s32[4,8]{1,0:T(4,128)} %param.25), kind=kLoop, calls=%fused_computation.72 | loop fusion | flops 256 | bytes 192 | tf_op jit(solution)/shard_map/ge | solution.py:30
  8.9 1.3 %compare_and_fusion = (pred[8,8]{1,0:T(8,128)(4,1)}, s32[8,8]{1,0:T(8,128)S(1)}, pred[8,8]{1,0:T(8,128)(4,1)}) fusion(s32[8,8]{1,0:T(8,128)} %param.24, s32[]{:T(128)S(6)} %mul.17), kind=kLoop, calls=%fused_computation.64 | loop fusion | flops 576 | bytes 644 | tf_op jit(solution)/shard_map/jit(_take)/and | solution.py:31
  10.3 1.6 %convolution_convert_fusion = bf16[32,64,16]{1,2,0:T(8,128)(2,1)S(1)} fusion(bf16[32,256,64]{1,2,0:T(8,128)(2,1)} %param.16, bf16[2,32,8,256]{3,2,1,0:T(8,128)(2,1)} %bitcast.75), kind=kOutput, calls=%fused_computation.11 | convolution fusion | flops 16809984 | bytes 1376256 | tf_op jit(solution)/shard_map/lpa,lpr->lar/dot_general | solution.py:67
  11.9 14.6 %all_gather.15 = bf16[256,64,16]{1,2,0:T(8,128)(2,1)S(1)} all-gather(bf16[32,64,16]{1,2,0:T(8,128)(2,1)S(1)} %convolution_convert_fusion), channel_id=1, replica_groups=mesh['row'=4,'col'=8] {'col'}, dimensions={0}, use_global_device_ids=true | all-gather | bytes 589824 | tf_op jit(solution)/shard_map/all_gather | solution.py:43
  26.6 1.3 %bitcast_reduce_fusion = bf16[16,64,16]{1,2,0:T(8,128)(2,1)S(1)} fusion(bf16[32,64,16]{1,2,0:T(8,128)(2,1)S(1)} %convolution_convert_fusion, bf16[32,64,64]{2,1,0:T(8,128)(2,1)} %param.19), kind=kOutput, calls=%fused_computation.35 | convolution fusion | flops 4210688 | bytes 360448 | tf_op jit(solution)/shard_map/cab,car->cbr/dot_general | solution.py:74
  27.9 10.0 %all_gather.16 = bf16[128,64,16]{1,2,0:T(8,128)(2,1)} all-gather(bf16[16,64,16]{1,2,0:T(8,128)(2,1)S(1)} %bitcast_reduce_fusion), channel_id=1, replica_groups=mesh['row'=4,'col'=8] {'col'}, dimensions={0}, use_global_device_ids=true | all-gather | bytes 294912 | tf_op jit(solution)/shard_map/all_gather | solution.py:43
  38.0 9.2 %all_gather.17 = bf16[64,64,16]{1,2,0:T(8,128)(2,1)S(1)} all-gather(bf16[8,64,16]{1,2,0:T(8,128)(2,1)S(1)} %bitcast_reduce_fusion.1), channel_id=1, replica_groups=mesh['row'=4,'col'=8] {'col'}, dimensions={0}, use_global_device_ids=true | all-gather | bytes 147456 | tf_op jit(solution)/shard_map/all_gather | solution.py:43
  47.4 8.3 %all_gather.18 = bf16[32,64,16]{1,2,0:T(8,128)(2,1)S(1)} all-gather(bf16[4,64,16]{1,2,0:T(8,128)(2,1)S(1)} %bitcast_reduce_fusion.2), channel_id=1, replica_groups=mesh['row'=4,'col'=8] {'col'}, dimensions={0}, use_global_device_ids=true | all-gather | bytes 73728 | tf_op jit(solution)/shard_map/all_gather | solution.py:80
  55.7 17.5 %all_gather.19 = bf16[128,64,16]{1,2,0:T(8,128)(2,1)} all-gather(bf16[32,64,16]{1,2,0:T(8,128)(2,1)S(1)} %all_gather.18), channel_id=1, replica_groups=mesh['row'=4,'col'=8] {'row'}, dimensions={0}, use_global_device_ids=true | all-gather | bytes 327680 | tf_op jit(solution)/shard_map/all_gather | solution.py:81
  74.1 0.7 copy.63
  75.8 1.3 %compare_and_fusion.3 = (pred[32,2]{0,1:T(4,128)(4,1)}, s32[32,2]{0,1:T(2,128)S(1)}, pred[32,2]{0,1:T(4,128)(4,1)}) fusion(s32[32,2]{0,1:T(2,128)} %param.17, s32[]{:T(128)S(6)} %mul.19), kind=kLoop, calls=%fused_computation.70 | loop fusion | flops 640 | bytes 644 | tf_op jit(solution)/shard_map/jit(_take)/and | solution.py:31
  77.1 0.7 reshape.102
  77.8 1.3 %gather_fusion.2 = bf16[64,64,16]{1,2,0:T(8,128)(2,1)} fusion(bf16[64,64,16]{1,2,0:T(8,128)(2,1)S(1)} %all_gather.17, s32[1024]{0:T(1024)S(1)} %pad_clamp_fusion.2), kind=kCustom, calls=%fused_computation.2 | custom fusion | bytes 262400 | tf_op jit(solution)/shard_map/jit(_take)/gather | solution.py:31
  79.1 1.6 %gather_fusion.3 = bf16[32,64,16]{1,2,0:T(8,128)(2,1)S(1)} fusion(bf16[128,64,16]{1,2,0:T(8,128)(2,1)} %all_gather.19, s32[1024]{0:T(1024)S(1)} %pad_clamp_fusion.1), kind=kCustom, calls=%fused_computation.3 | custom fusion | bytes 131200 | tf_op jit(solution)/shard_map/jit(_take)/gather | solution.py:31
  80.8 1.8 %convolution_bitcast_fusion.3 = f32[8,16,64]{2,1,0:T(8,128)S(1)} fusion(bf16[8,8,64,64]{3,2,1,0:T(8,128)(2,1)} %param.28, bf16[8,8,64,16]{2,3,1,0:T(8,128)(2,1)} %bitcast.73, pred[8,8]{1,0:T(8,128)(4,1)} %get-tuple-element.5, pred[8,8]{1,0:T(8,128)(4,1)} %get-tuple-element.15), kind=kOutput, calls=%fused_computation.17 | convolution fusion | flops 8519680 | bytes 688256 | tf_op jit(solution)/shard_map/enyd,endc->eyc/dot_general | solution.py:37
  82.5 1.4 %convolution_bitcast_fusion.4 = f32[4,64,16]{1,2,0:T(8,128)S(1)} fusion(bf16[4,8,64,64]{3,2,1,0:T(8,128)(2,1)} %param.29, bf16[4,8,64,16]{2,3,1,0:T(8,128)(2,1)S(1)} %bitcast.74, pred[4,8]{1,0:T(4,128)(4,1)} %get-tuple-element.19, pred[4,8]{1,0:T(4,128)(4,1)} %get-tuple-element.18), kind=kOutput, calls=%fused_computation.18 | convolution fusion | flops 4259840 | bytes 344128 | tf_op jit(solution)/shard_map/enyd,endc->eyc/dot_general | solution.py:37
  84.0 1.2 %fusion.3 = f32[8,64,16]{1,2,0:T(8,128)S(1)} fusion(f32[8,16,64]{2,1,0:T(8,128)S(1)} %convolution_bitcast_fusion.3, f32[8,64,16]{1,2,0:T(8,128)S(1)} %bitcast.80, bf16[8,64,64]{2,1,0:T(8,128)(2,1)} %param.21), kind=kOutput, calls=%fused_computation.16 | convolution fusion | flops 6299648 | bytes 163840 | tf_op jit(solution)/shard_map/cab,cbr->car/dot_general | solution.py:97
  85.2 2.5 %gather_fusion.1 = bf16[128,64,16]{1,2,0:T(8,128)(2,1)} fusion(bf16[128,64,16]{1,2,0:T(8,128)(2,1)} %all_gather.16, s32[1024]{0:T(1024)S(1)} %pad_clamp_fusion.3), kind=kCustom, calls=%fused_computation.1 | custom fusion | bytes 524800 | tf_op jit(solution)/shard_map/jit(_take)/gather | solution.py:31
  87.7 1.8 %convolution_bitcast_fusion.2 = f32[16,16,64]{2,1,0:T(8,128)S(1)} fusion(bf16[16,8,64,64]{3,2,1,0:T(8,128)(2,1)S(1)} %copy-done, bf16[16,8,64,16]{2,3,1,0:T(8,128)(2,1)} %bitcast.72, pred[16,8]{1,0:T(8,128)(4,1)} %copy.63, pred[16,8]{1,0:T(8,128)(4,1)S(1)} %copy-done.13), kind=kOutput, calls=%fused_computation.14 | convolution fusion | flops 17039360 | bytes 1376512 | tf_op jit(solution)/shard_map/enyd,endc->eyc/dot_general | solution.py:37
  90.0 1.8 %gather_fusion = bf16[256,64,16]{1,2,0:T(8,128)(2,1)} fusion(bf16[256,64,16]{1,2,0:T(8,128)(2,1)S(1)} %all_gather.15, s32[1024]{0:T(1024)S(1)} %pad_clamp_fusion.4), kind=kCustom, calls=%fused_computation | custom fusion | bytes 1049600 | tf_op jit(solution)/shard_map/jit(_take)/gather | solution.py:31
  91.8 3.3 %convolution_bitcast_fusion.1 = f32[32,16,64]{2,1,0:T(8,128)S(1)} fusion(bf16[32,8,64,64]{3,2,1,0:T(8,128)(2,1)} %param.26, bf16[32,8,64,16]{2,3,1,0:T(8,128)(2,1)} %bitcast.71, pred[32,8]{1,0:T(8,128)(4,1)S(1)} %copy-done.7, pred[32,8]{1,0:T(8,128)(4,1)S(1)} %copy.58), kind=kOutput, calls=%fused_computation.9 | convolution fusion | flops 34078720 | bytes 2753024 | tf_op jit(solution)/shard_map/enyd,endc->eyc/dot_general | solution.py:37
  95.2 0.9 convolution_add_fusion.1
  96.4 0.9 concatenate.8
  97.4 0.9 concatenate.9
  99.0 5.8 %convolution_bitcast_fusion = f32[32,16,256]{2,1,0:T(8,128)S(1)} fusion(bf16[32,2,256,256]{3,2,1,0:T(8,128)(2,1)} %param.18, bf16[32,2,256,16]{2,3,1,0:T(8,128)(2,1)S(1)} %bitcast.70, pred[32,2]{1,0:T(8,128)(4,1)S(1)} %copy.66, pred[32,2]{1,0:T(8,128)(4,1)S(1)} %copy.65), kind=kOutput, calls=%fused_computation.6 | convolution fusion | flops 134742016 | bytes 9437312 | tf_op jit(solution)/shard_map/iknm,ikmr->inr/dot_general | solution.py:108
  105.4 0.7 copy.80
  (63 shorter events, 4.9 us)
Async XLA Ops:
  0.0 87.7 %copy-start = (bf16[16,8,64,64]{3,2,1,0:T(8,128)(2,1)S(1)}, bf16[16,8,64,64]{3,2,1,0:T(8,128)(2,1)}, u32[]{:S(2)}) copy-start(bf16[16,8,64,64]{3,2,1,0:T(8,128)(2,1)} %param.27) | copy-start | bytes 3145732
  0.0 37.8 %copy-start.4 = (bf16[16,64,64]{2,1,0:T(8,128)(2,1)S(1)}, bf16[16,64,64]{2,1,0:T(8,128)(2,1)}, u32[]{:S(2)}) copy-start(bf16[16,64,64]{2,1,0:T(8,128)(2,1)} %param.20) | copy-start | bytes 393220
  0.0 47.2 %copy-start.6 = (bf16[8,64,64]{2,1,0:T(8,128)(2,1)S(1)}, bf16[8,64,64]{2,1,0:T(8,128)(2,1)}, u32[]{:S(2)}) copy-start(bf16[8,64,64]{2,1,0:T(8,128)(2,1)} %param.21) | copy-start | bytes 196612
  0.0 73.3 %copy-start.8 = (s32[16,8]{0,1:T(8,128)S(1)}, s32[16,8]{0,1:T(8,128)}, u32[]{:S(2)}) copy-start(s32[16,8]{0,1:T(8,128)} %param.23) | copy-start | bytes 1540
  0.0 74.8 %copy-start.9 = (s32[32,8]{0,1:T(8,128)S(1)}, s32[32,8]{0,1:T(8,128)}, u32[]{:S(2)}) copy-start(s32[32,8]{0,1:T(8,128)} %param.22) | copy-start | bytes 3076
  1.8 94.6 %collective-permute-start = (bf16[2,4096]{1,0:T(2,128)(2,1)}, bf16[2,4096]{1,0:T(2,128)(2,1)}, u32[]{:S(2)}, u32[]{:S(2)}) collective-permute-start(bf16[2,4096]{1,0:T(2,128)(2,1)} %slice.13), channel_id=1, source_target_pairs={{0,1},{1,2},{2,3},{3,4},{4,5},{5,6},{6,7},{7,8},{8,9},{9,10},{10,1... | collective-permute-start | bytes 49160 | tf_op jit(solution)/shard_map/ppermute | solution.py:20
  5.7 91.7 %collective-permute-start.1 = (bf16[2,4096]{1,0:T(2,128)(2,1)}, bf16[2,4096]{1,0:T(2,128)(2,1)}, u32[]{:S(2)}, u32[]{:S(2)}) collective-permute-start(bf16[2,4096]{1,0:T(2,128)(2,1)} %slice.15), channel_id=1, source_target_pairs={{1,0},{2,1},{3,2},{4,3},{5,4},{6,5},{7,6},{8,7},{9,8},{10,9},{11,1... | collective-permute-start | bytes 49160 | tf_op jit(solution)/shard_map/ppermute | solution.py:22
  79.1 8.6 %copy-start.13 = (pred[16,8]{1,0:T(8,128)(4,1)S(1)}, pred[16,8]{1,0:T(8,128)(4,1)}, u32[]{:S(2)}) copy-start(pred[16,8]{1,0:T(8,128)(4,1)} %copy.62) | copy-start | bytes 388
  82.5 7.0 %copy-start.5 = (bf16[16,64,64]{2,1,0:T(8,128)(2,1)S(1)}, bf16[16,64,64]{2,1,0:T(8,128)(2,1)}, u32[]{:S(2)}) copy-start(bf16[16,64,64]{2,1,0:T(8,128)(2,1)} %param.20) | copy-start | bytes 393220
  90.0 1.8 %copy-start.7 = (pred[32,8]{1,0:T(8,128)(4,1)S(1)}, pred[32,8]{1,0:T(8,128)(4,1)}, u32[]{:S(2)}) copy-start(pred[32,8]{1,0:T(8,128)(4,1)} %copy.59) | copy-start | bytes 772
  91.8 3.4 %copy-start.2 = (bf16[32,64,64]{2,1,0:T(8,128)(2,1)S(1)}, bf16[32,64,64]{2,1,0:T(8,128)(2,1)}, u32[]{:S(2)}) copy-start(bf16[32,64,64]{2,1,0:T(8,128)(2,1)} %param.19) | copy-start | bytes 786436
  91.8 4.4 %copy-start.12 = (s32[64]{0:T(128)S(1)}, s32[64]{0:T(128)}, u32[]{:S(2)}) copy-start(s32[64]{0:T(128)} %reshape.102) | copy-start | bytes 772
  91.8 4.4 %copy-start.3 = (bf16[8192,16]{0,1:T(8,128)(2,1)S(1)}, bf16[8192,16]{0,1:T(8,128)(2,1)}, u32[]{:S(2)}) copy-start(bf16[8192,16]{0,1:T(8,128)(2,1)} %param.15) | copy-start | bytes 786436
  91.8 4.4 %copy-start.11 = (pred[32,2]{0,1:T(4,128)(4,1)S(1)}, pred[32,2]{0,1:T(4,128)(4,1)}, u32[]{:S(2)}) copy-start(pred[32,2]{0,1:T(4,128)(4,1)} %get-tuple-element.20) | copy-start | bytes 196
  91.8 4.5 %copy-start.10 = (pred[32,2]{0,1:T(4,128)(4,1)S(1)}, pred[32,2]{0,1:T(4,128)(4,1)}, u32[]{:S(2)}) copy-start(pred[32,2]{0,1:T(4,128)(4,1)} %get-tuple-element.11) | copy-start | bytes 196
  99.0 5.8 %copy-start.1 = (bf16[32,256,64]{1,2,0:T(8,128)(2,1)S(1)}, bf16[32,256,64]{1,2,0:T(8,128)(2,1)}, u32[]{:S(2)}) copy-start(bf16[32,256,64]{1,2,0:T(8,128)(2,1)} %param.16) | copy-start | bytes 3145732
where the time goes:
time: 107 us; the launch traced here: 106 us
  blocking collectives  59.6 us (56%)
  matrix products  20.5 us (19%)
  local copies, waits for them, and re-layouts  16.8 us (16%)
  other arithmetic  4.61 us (4%)
  starting transfers between devices  4.27 us (4%)
    all_gather x3, blocking collectives, collect_group(): return lax.all_gather(skeleton, 'col', axis=0, tiled=True)  33.8 us
    all_gather x1, blocking collectives, shards(): coarse_table = lax.all_gather(coarse_group, 'row', axis=0, tiled=True)  17.5 us
    all_gather x1, blocking collectives, shards(): coarse_group = lax.all_gather(skeletons[3], 'col', axis=0, tiled=True)  8.34 us
    dot_general x4, matrix products, couple_level(): jnp.einsum('enyd,endc->eyc', coupling_block, selected_rows, preferred_ele...  8.29 us
    gather x5, local copies, waits for them, and re-layouts, gather_active(): jnp.take(table, jnp.clip(local_ids, 0, table.shape[0] - 1), axis=0)  7.86 us
    dot_general x1, matrix products, shards(): jnp.einsum('iknm,ikmr->inr', near_blocks, near_picked, preferred_element_...  5.76 us
    ppermute x1, starting transfers between devices, padded_2(): lax.ppermute(tail, axis, [(i, (i + 1) % count) for i in range(ends)])  2.99 us
    dot_general x3, matrix products, shards(): jnp.einsum('cab,cbr->car', transfers[level_index - 1].astype(jnp.float32)...  2.64 us
  transfers between devices with their start and end apart: 2, of which 0 were waited for; matrix products, arithmetic and copies ran while one was open for 30% of the time, Pallas kernels for 0%

commit v1 on v0

--- a/solution.py
+++ b/solution.py
@@ -40,7 +40,9 @@
 
 
 def collect_group(skeleton):
-    return lax.all_gather(skeleton, "col", axis=0, tiled=True)
+    return jnp.concatenate(
+        lax.all_to_all(jnp.stack([skeleton] * lax.axis_size("col")), "col", 0, 0), axis=0
+    )
 
 
 def shards(

time: 107 us -> 116 us (1.084)
  blocking collectives: 59.6 us -> 28.8 us
  starting transfers between devices: 4.27 us -> 17.2 us
  local copies, waits for them, and re-layouts: 16.8 us -> 28 us
  waiting for transfers between devices: 0.01 us -> 9.57 us
  other arithmetic: 4.61 us -> 8.06 us
  matrix products: 20.5 us -> 22.7 us
    all_gather x3 -> x0, blocking collectives: 33.8 us -> none  [collect_group(): return lax.all_gather(skeleton, 'col', axis=0, tiled=True)]
    all_to_all x0 -> x3, starting transfers between devices: none -> 12.9 us  [collect_group(): lax.all_to_all(jnp.stack([skeleton] * lax.axis_size('col')), 'col', 0, 0)]
    all_to_all x0 -> x3, waiting for transfers between devices: none -> 9.56 us  [collect_group(): lax.all_to_all(jnp.stack([skeleton] * lax.axis_size('col')), 'col', 0, 0)]
    unnamed x28 -> x37, local copies, waits for them, and re-layouts: 0.06 us -> 9.37 us
    all_gather x1, blocking collectives: 8.34 us -> 11.9 us  [shards(): coarse_group = lax.all_gather(skeletons[3], 'col', axis=0, tiled=True)]
    gather x5, local copies, waits for them, and re-layouts: 7.86 us -> 5.32 us  [gather_active(): jnp.take(table, jnp.clip(local_ids, 0, table.shape[0] - 1), axis=0)]
    ge x3, local copies, waits for them, and re-layouts: 0.85 us -> 2.82 us  [gather_active(): is_live = sources >= 0]
    and x3, local copies, waits for them, and re-layouts: 1.44 us -> 3.38 us  [gather_active(): jnp.take(table, jnp.clip(local_ids, 0, table.shape[0] - 1), axis=0)]
  transfers between devices with their start and end apart: 2 -> 5, of which waited for: 0 -> 2; matrix products, arithmetic and copies ran while one was open for 30% -> 38% of each run, Pallas kernels for 0% -> 0%
where the time goes in v1:
time: 116 us; the launch traced here: 115 us
  blocking collectives  28.8 us (25%)
  local copies, waits for them, and re-layouts  28 us (24%)
  matrix products  22.7 us (20%)
  starting transfers between devices  17.2 us (15%)
  waiting for transfers between devices  9.57 us (8%)
  other arithmetic  8.06 us (7%)
    all_gather x1, blocking collectives, shards(): coarse_table = lax.all_gather(coarse_group, 'row', axis=0, tiled=True)  16.9 us
    all_to_all x3, starting transfers between devices, collect_group(): lax.all_to_all(jnp.stack([skeleton] * lax.axis_size('col')), 'col', 0, 0)  12.9 us
    all_gather x1, blocking collectives, shards(): coarse_group = lax.all_gather(skeletons[3], 'col', axis=0, tiled=True)  11.9 us
    all_to_all x3, waiting for transfers between devices, collect_group(): lax.all_to_all(jnp.stack([skeleton] * lax.axis_size('col')), 'col', 0, 0)  9.56 us
    unnamed x37, local copies, waits for them, and re-layouts  9.37 us
    dot_general x4, matrix products, couple_level(): jnp.einsum('enyd,endc->eyc', coupling_block, selected_rows, preferred_ele...  8.64 us
    dot_general x1, matrix products, shards(): jnp.einsum('iknm,ikmr->inr', near_blocks, near_picked, preferred_element_...  6.5 us
    gather x5, local copies, waits for them, and re-layouts, gather_active(): jnp.take(table, jnp.clip(local_ids, 0, table.shape[0] - 1), axis=0)  5.32 us
  transfers between devices with their start and end apart: 5, of which 2 were waited for; matrix products, arithmetic and copies ran while one was open for 38% of the time, Pallas kernels for 0%

profile of v1, /device:TPU:0, one launch (start us, length us, event | category | flops | bytes accessed | tf_op | source)
XLA Modules:
  0.0 114.7 jit_solution(11879117641498539146)
XLA Ops:
  0.0 1.8 %convolution_convert_fusion = bf16[32,64,16]{1,2,0:T(8,128)(2,1)S(1)} fusion(bf16[32,256,64]{1,2,0:T(8,128)(2,1)} %param.16, bf16[2,32,8,256]{3,2,1,0:T(8,128)(2,1)} %bitcast.90), kind=kOutput, calls=%fused_computation.11 | convolution fusion | flops 16809984 | bytes 1376256 | tf_op jit(solution)/shard_map/lpa,lpr->lar/dot_general | solution.py:69
  1.8 1.3 %bitcast_reduce_fusion = bf16[16,64,16]{1,2,0:T(8,128)(2,1)S(1)} fusion(bf16[32,64,16]{1,2,0:T(8,128)(2,1)S(1)} %convolution_convert_fusion, bf16[32,64,64]{2,1,0:T(8,128)(2,1)} %param.19), kind=kOutput, calls=%fused_computation.35 | convolution fusion | flops 4210688 | bytes 360448 | tf_op jit(solution)/shard_map/cab,car->cbr/dot_general | solution.py:76
  3.1 1.1 bitcast_reduce_fusion.1
  5.2 5.2 %all-to-all-start.2 = ((bf16[8,2,4096]{2,1,0:T(2,128)(2,1)}), bf16[8,2,4096]{2,1,0:T(2,128)(2,1)}, u32[]{:S(2)}, u32[]{:S(2)}) async-start(bf16[8,2,4096]{2,1,0:T(2,128)(2,1)} %reshape.145), calls=%async_computation.2 | async-start | bytes 262144 | tf_op jit(solution)/shard_map/all_to_all | solution.py:44
  12.0 3.0 %collective-permute-start = (bf16[2,4096]{1,0:T(2,128)(2,1)}, bf16[2,4096]{1,0:T(2,128)(2,1)}, u32[]{:S(2)}, u32[]{:S(2)}) collective-permute-start(bf16[2,4096]{1,0:T(2,128)(2,1)} %slice.13), channel_id=1, source_target_pairs={{0,1},{1,2},{2,3},{3,4},{4,5},{5,6},{6,7},{7,8},{8,9},{9,10},{10,1... | collective-permute-start | bytes 49160 | tf_op jit(solution)/shard_map/ppermute | solution.py:20
  15.9 1.3 %collective-permute-start.1 = (bf16[2,4096]{1,0:T(2,128)(2,1)}, bf16[2,4096]{1,0:T(2,128)(2,1)}, u32[]{:S(2)}, u32[]{:S(2)}) collective-permute-start(bf16[2,4096]{1,0:T(2,128)(2,1)} %slice.15), channel_id=1, source_target_pairs={{1,0},{2,1},{3,2},{4,3},{5,4},{6,5},{7,6},{8,7},{9,8},{10,9},{11,1... | collective-permute-start | bytes 49160 | tf_op jit(solution)/shard_map/ppermute | solution.py:22
  17.9 1.3 %broadcast_compare_fusion.3 = (pred[4,8]{1,0:T(4,128)(4,1)}, pred[4,8]{1,0:T(4,128)(4,1)}) fusion(s32[4,8]{1,0:T(4,128)} %param.25), kind=kLoop, calls=%fused_computation.72 | loop fusion | flops 256 | bytes 192 | tf_op jit(solution)/shard_map/ge | solution.py:30
  20.9 1.1 bitcast_reduce_fusion.2
  22.0 11.9 %all_gather.6 = bf16[32,64,16]{1,2,0:T(8,128)(2,1)S(1)} all-gather(bf16[4,64,16]{1,2,0:T(8,128)(2,1)S(1)} %bitcast_reduce_fusion.2), channel_id=1, replica_groups=mesh['row'=4,'col'=8] {'col'}, dimensions={0}, use_global_device_ids=true | all-gather | bytes 73728 | tf_op jit(solution)/shard_map/all_gather | solution.py:82
  33.9 16.9 %all_gather.7 = bf16[128,64,16]{1,2,0:T(8,128)(2,1)} all-gather(bf16[32,64,16]{1,2,0:T(8,128)(2,1)S(1)} %all_gather.6), channel_id=1, replica_groups=mesh['row'=4,'col'=8] {'row'}, dimensions={0}, use_global_device_ids=true | all-gather | bytes 327680 | tf_op jit(solution)/shard_map/all_gather | solution.py:83
  50.9 1.3 %compare_and_fusion.1 = (pred[16,8]{0,1:T(8,128)(4,1)}, s32[16,8]{0,1:T(8,128)S(1)}, pred[16,8]{0,1:T(8,128)(4,1)}) fusion(s32[16,8]{0,1:T(8,128)} %param.23, s32[]{:T(128)S(6)} %mul.16), kind=kLoop, calls=%fused_computation.65 | loop fusion | flops 1152 | bytes 1284 | tf_op jit(solution)/shard_map/jit(_take)/and | solution.py:31
  52.3 1.3 %compare_and_fusion.2 = (pred[32,8]{0,1:T(8,128)(4,1)}, s32[32,8]{0,1:T(8,128)S(1)}, pred[32,8]{0,1:T(8,128)(4,1)}) fusion(s32[32,8]{0,1:T(8,128)} %param.22, s32[]{:T(128)S(6)} %mul.15), kind=kLoop, calls=%fused_computation.66 | loop fusion | flops 2304 | bytes 2564 | tf_op jit(solution)/shard_map/jit(_take)/and | solution.py:31
  53.8 1.3 %compare_and_fusion.3 = (pred[32,2]{0,1:T(4,128)(4,1)}, s32[32,2]{0,1:T(2,128)S(1)}, pred[32,2]{0,1:T(4,128)(4,1)}) fusion(s32[32,2]{0,1:T(2,128)} %param.17, s32[]{:T(128)S(6)} %mul.19), kind=kLoop, calls=%fused_computation.70 | loop fusion | flops 640 | bytes 644 | tf_op jit(solution)/shard_map/jit(_take)/and | solution.py:31
  55.7 1.6 %gather_fusion.3 = bf16[32,64,16]{1,2,0:T(8,128)(2,1)S(1)} fusion(bf16[128,64,16]{1,2,0:T(8,128)(2,1)} %all_gather.7, s32[1024]{0:T(1024)S(1)} %pad_clamp_fusion.1), kind=kCustom, calls=%fused_computation.3 | custom fusion | bytes 131200 | tf_op jit(solution)/shard_map/jit(_take)/gather | solution.py:31
  57.4 2.0 %convolution_bitcast_fusion.4 = f32[4,64,16]{1,2,0:T(8,128)} fusion(bf16[4,8,64,64]{3,2,1,0:T(8,128)(2,1)} %param.29, bf16[4,8,64,16]{2,3,1,0:T(8,128)(2,1)S(1)} %bitcast.89, pred[4,8]{1,0:T(4,128)(4,1)} %get-tuple-element.19, pred[4,8]{1,0:T(4,128)(4,1)} %get-tuple-element.18), kind=kOutput, calls=%fused_computation.18 | convolution fusion | flops 4259840 | bytes 344128 | tf_op jit(solution)/shard_map/enyd,endc->eyc/dot_general | solution.py:37
  60.7 2.1 %reshape.143 = bf16[8,2,8192]{2,1,0:T(2,128)(2,1)} reshape(bf16[8,16,16,64]{3,2,1,0:T(8,128)(2,1)} %broadcast_bitcast_fusion.1) | data formatting | bytes 524288
  62.9 1.3 %copy.83 = pred[16,8]{1,0:T(8,128)(4,1)} copy(pred[16,8]{0,1:T(8,128)(4,1)} %get-tuple-element.16) | data formatting | bytes 256 | tf_op jit(solution)/shard_map/ge | solution.py:30
  64.2 1.3 %copy.84 = pred[16,8]{1,0:T(8,128)(4,1)} copy(pred[16,8]{0,1:T(8,128)(4,1)} %get-tuple-element.7) | data formatting | bytes 256 | tf_op jit(solution)/shard_map/jit(_take)/and | solution.py:31
  65.5 1.5 %reshape.141 = bf16[8,2,16384]{2,1,0:T(2,128)(2,1)} reshape(bf16[8,32,16,64]{3,2,1,0:T(8,128)(2,1)S(1)} %broadcast_bitcast_fusion) | data formatting | bytes 1048576
  67.8 1.3 %copy.80 = pred[32,8]{1,0:T(8,128)(4,1)} copy(pred[32,8]{0,1:T(8,128)(4,1)} %get-tuple-element.9) | data formatting | bytes 512 | tf_op jit(solution)/shard_map/jit(_take)/and | solution.py:31
  72.5 1.0 pad_maximum_fusion
  74.1 6.5 %convolution_bitcast_fusion = f32[32,16,256]{2,1,0:T(8,128)} fusion(bf16[32,2,256,256]{3,2,1,0:T(8,128)(2,1)} %param.18, bf16[32,2,256,16]{2,3,1,0:T(8,128)(2,1)S(1)} %bitcast.82, pred[32,2]{1,0:T(8,128)(4,1)S(1)} %copy.87, pred[32,2]{1,0:T(8,128)(4,1)S(1)} %copy.86), kind=kOutput, calls=%fused_computation.6 | convolution fusion | flops 134742016 | bytes 9437312 | tf_op jit(solution)/shard_map/iknm,ikmr->inr/dot_general | solution.py:110
  80.6 3.5 %all-to-all-start.1 = ((bf16[8,2,8192]{2,1,0:T(2,128)(2,1)}), bf16[8,2,8192]{2,1,0:T(2,128)(2,1)S(1)}, u32[]{:S(2)}, u32[]{:S(2)}) async-start(bf16[8,2,8192]{2,1,0:T(2,128)(2,1)} %reshape.143), calls=%async_computation.1 | async-start | bytes 524288 | tf_op jit(solution)/shard_map/all_to_all | solution.py:44
  84.2 1.1 reshape.146
  86.0 1.7 %convolution_bitcast_fusion.3 = f32[8,16,64]{2,1,0:T(8,128)S(1)} fusion(bf16[8,8,64,64]{3,2,1,0:T(8,128)(2,1)} %param.28, bf16[8,8,64,16]{2,3,1,0:T(8,128)(2,1)S(1)} %bitcast.88, pred[8,8]{1,0:T(8,128)(4,1)S(1)} %copy-done.12, pred[8,8]{1,0:T(8,128)(4,1)S(1)} %copy-done.13), kind=kOutput, calls=%fused_computation.17 | convolution fusion | flops 8519680 | bytes 688256 | tf_op jit(solution)/shard_map/enyd,endc->eyc/dot_general | solution.py:37
  88.0 3.1 %all-to-all-done.1 = bf16[8,2,8192]{2,1,0:T(2,128)(2,1)S(1)} async-done(((bf16[8,2,8192]{2,1,0:T(2,128)(2,1)}), bf16[8,2,8192]{2,1,0:T(2,128)(2,1)S(1)}, u32[]{:S(2)}, u32[]{:S(2)}) %all-to-all-start.1) | async-done | bytes 262176 | tf_op jit(solution)/shard_map/all_to_all | solution.py:44
  91.0 4.1 %all-to-all-start = ((bf16[8,2,16384]{2,1,0:T(2,128)(2,1)}), bf16[8,2,16384]{2,1,0:T(2,128)(2,1)}, u32[]{:S(2)}, u32[]{:S(2)}) async-start(bf16[8,2,16384]{2,1,0:T(2,128)(2,1)} %reshape.141), calls=%async_computation | async-start | bytes 1048576 | tf_op jit(solution)/shard_map/all_to_all | solution.py:44
  96.3 1.6 %convolution_bitcast_fusion.2 = f32[16,16,64]{2,1,0:T(8,128)S(1)} fusion(bf16[16,8,64,64]{3,2,1,0:T(8,128)(2,1)S(1)} %copy-done, bf16[16,8,64,16]{2,3,1,0:T(8,128)(2,1)S(1)} %bitcast.86, pred[16,8]{1,0:T(8,128)(4,1)} %copy.84, pred[16,8]{1,0:T(8,128)(4,1)S(1)} %copy-done.11), kind=kOutput, calls=%fused_computation.14 | convolution fusion | flops 17039360 | bytes 1376512 | tf_op jit(solution)/shard_map/enyd,endc->eyc/dot_general | solution.py:37
  98.4 6.5 %all-to-all-done = bf16[8,2,16384]{2,1,0:T(2,128)(2,1)} async-done(((bf16[8,2,16384]{2,1,0:T(2,128)(2,1)}), bf16[8,2,16384]{2,1,0:T(2,128)(2,1)}, u32[]{:S(2)}, u32[]{:S(2)}) %all-to-all-start) | async-done | bytes 524320 | tf_op jit(solution)/shard_map/all_to_all | solution.py:44
  104.9 2.3 %reshape.142 = bf16[8,32,16,64]{3,2,1,0:T(8,128)(2,1)S(1)} reshape(bf16[8,2,16384]{2,1,0:T(2,128)(2,1)} %all-to-all-done) | data formatting | bytes 1048576
  107.2 1.8 %gather_fusion = bf16[256,64,16]{1,2,0:T(8,128)(2,1)} fusion(bf16[256,64,16]{1,2,0:T(8,128)(2,1)S(1)} %bitcast.83, s32[1024]{0:T(1024)S(1)} %pad_clamp_fusion.4), kind=kCustom, calls=%fused_computation | custom fusion | bytes 1049600 | tf_op jit(solution)/shard_map/jit(_take)/gather | solution.py:31
  109.0 3.4 %convolution_bitcast_fusion.1 = f32[32,16,64]{2,1,0:T(8,128)S(1)} fusion(bf16[32,8,64,64]{3,2,1,0:T(8,128)(2,1)} %param.26, bf16[32,8,64,16]{2,3,1,0:T(8,128)(2,1)} %bitcast.84, pred[32,8]{1,0:T(8,128)(4,1)S(1)} %copy-done.9, pred[32,8]{1,0:T(8,128)(4,1)S(1)} %copy.79), kind=kOutput, calls=%fused_computation.9 | convolution fusion | flops 34078720 | bytes 2753024 | tf_op jit(solution)/shard_map/enyd,endc->eyc/dot_general | solution.py:37
  (75 shorter events, 17.9 us)
Async XLA Ops:
  0.0 96.3 %copy-start = (bf16[16,8,64,64]{3,2,1,0:T(8,128)(2,1)S(1)}, bf16[16,8,64,64]{3,2,1,0:T(8,128)(2,1)}, u32[]{:S(2)}) copy-start(bf16[16,8,64,64]{3,2,1,0:T(8,128)(2,1)} %param.27) | copy-start | bytes 3145732
  0.0 20.2 %copy-start.10 = (s32[8,8]{1,0:T(8,128)S(1)}, s32[8,8]{1,0:T(8,128)}, u32[]{:S(2)}) copy-start(s32[8,8]{1,0:T(8,128)} %param.24) | copy-start | bytes 772
  0.0 60.0 %copy-start.4 = (bf16[8192,16]{0,1:T(8,128)(2,1)S(1)}, bf16[8192,16]{0,1:T(8,128)(2,1)}, u32[]{:S(2)}) copy-start(bf16[8192,16]{0,1:T(8,128)(2,1)} %param.15) | copy-start | bytes 786436
  4.3 14.9 %copy-start.7 = (bf16[8,64,16]{1,2,0:T(8,128)(2,1)}, bf16[8,64,16]{1,2,0:T(8,128)(2,1)S(1)}, u32[]{:S(2)}) copy-start(bf16[8,64,16]{1,2,0:T(8,128)(2,1)S(1)} %bitcast_reduce_fusion.1) | copy-start | bytes 49156
  5.2 75.4 %all-to-all-start.2 = ((bf16[8,2,4096]{2,1,0:T(2,128)(2,1)}), bf16[8,2,4096]{2,1,0:T(2,128)(2,1)}, u32[]{:S(2)}, u32[]{:S(2)}) async-start(bf16[8,2,4096]{2,1,0:T(2,128)(2,1)} %reshape.145), calls=%async_computation.2 | async-start | bytes 262144 | tf_op jit(solution)/shard_map/all_to_all | solution.py:44
  12.0 58.5 %collective-permute-start = (bf16[2,4096]{1,0:T(2,128)(2,1)}, bf16[2,4096]{1,0:T(2,128)(2,1)}, u32[]{:S(2)}, u32[]{:S(2)}) collective-permute-start(bf16[2,4096]{1,0:T(2,128)(2,1)} %slice.13), channel_id=1, source_target_pairs={{0,1},{1,2},{2,3},{3,4},{4,5},{5,6},{6,7},{7,8},{8,9},{9,10},{10,1... | collective-permute-start | bytes 49160 | tf_op jit(solution)/shard_map/ppermute | solution.py:20
  15.9 55.6 %collective-permute-start.1 = (bf16[2,4096]{1,0:T(2,128)(2,1)}, bf16[2,4096]{1,0:T(2,128)(2,1)}, u32[]{:S(2)}, u32[]{:S(2)}) collective-permute-start(bf16[2,4096]{1,0:T(2,128)(2,1)} %slice.15), channel_id=1, source_target_pairs={{1,0},{2,1},{3,2},{4,3},{5,4},{6,5},{7,6},{8,7},{9,8},{10,9},{11,1... | collective-permute-start | bytes 49160 | tf_op jit(solution)/shard_map/ppermute | solution.py:22
  74.1 11.8 %copy-start.12 = (pred[8,8]{1,0:T(8,128)(4,1)S(1)}, pred[8,8]{1,0:T(8,128)(4,1)}, u32[]{:S(2)}) copy-start(pred[8,8]{1,0:T(8,128)(4,1)} %get-tuple-element.5) | copy-start | bytes 196
  74.1 11.8 %copy-start.13 = (pred[8,8]{1,0:T(8,128)(4,1)S(1)}, pred[8,8]{1,0:T(8,128)(4,1)}, u32[]{:S(2)}) copy-start(pred[8,8]{1,0:T(8,128)(4,1)} %get-tuple-element.15) | copy-start | bytes 196
  80.6 7.0 %copy-start.8 = (f32[4,64,16]{1,2,0:T(8,128)S(1)}, f32[4,64,16]{1,2,0:T(8,128)}, u32[]{:S(2)}) copy-start(f32[4,64,16]{1,2,0:T(8,128)} %convolution_bitcast_fusion.4) | copy-start | bytes 49156
  80.6 7.0 %copy-start.6 = (bf16[8,64,64]{2,1,0:T(8,128)(2,1)S(1)}, bf16[8,64,64]{2,1,0:T(8,128)(2,1)}, u32[]{:S(2)}) copy-start(bf16[8,64,64]{2,1,0:T(8,128)(2,1)} %param.21) | copy-start | bytes 196612
  80.6 10.4 %all-to-all-start.1 = ((bf16[8,2,8192]{2,1,0:T(2,128)(2,1)}), bf16[8,2,8192]{2,1,0:T(2,128)(2,1)S(1)}, u32[]{:S(2)}, u32[]{:S(2)}) async-start(bf16[8,2,8192]{2,1,0:T(2,128)(2,1)} %reshape.143), calls=%async_computation.1 | async-start | bytes 524288 | tf_op jit(solution)/shard_map/all_to_all | solution.py:44
  85.9 10.3 %copy-start.11 = (pred[16,8]{1,0:T(8,128)(4,1)S(1)}, pred[16,8]{1,0:T(8,128)(4,1)}, u32[]{:S(2)}) copy-start(pred[16,8]{1,0:T(8,128)(4,1)} %copy.83) | copy-start | bytes 388
  91.0 13.9 %all-to-all-start = ((bf16[8,2,16384]{2,1,0:T(2,128)(2,1)}), bf16[8,2,16384]{2,1,0:T(2,128)(2,1)}, u32[]{:S(2)}, u32[]{:S(2)}) async-start(bf16[8,2,16384]{2,1,0:T(2,128)(2,1)} %reshape.141), calls=%async_computation | async-start | bytes 1048576 | tf_op jit(solution)/shard_map/all_to_all | solution.py:44
  95.2 2.7 %copy-start.5 = (bf16[16,64,64]{2,1,0:T(8,128)(2,1)S(1)}, bf16[16,64,64]{2,1,0:T(8,128)(2,1)}, u32[]{:S(2)}) copy-start(bf16[16,64,64]{2,1,0:T(8,128)(2,1)} %param.20) | copy-start | bytes 393220
  107.2 1.8 %copy-start.9 = (pred[32,8]{1,0:T(8,128)(4,1)S(1)}, pred[32,8]{1,0:T(8,128)(4,1)}, u32[]{:S(2)}) copy-start(pred[32,8]{1,0:T(8,128)(4,1)} %copy.80) | copy-start | bytes 772
  109.0 3.5 %copy-start.2 = (bf16[32,64,64]{2,1,0:T(8,128)(2,1)S(1)}, bf16[32,64,64]{2,1,0:T(8,128)(2,1)}, u32[]{:S(2)}) copy-start(bf16[32,64,64]{2,1,0:T(8,128)(2,1)} %param.19) | copy-start | bytes 786436
  109.0 4.4 %copy-start.1 = (bf16[32,256,64]{1,2,0:T(8,128)(2,1)S(1)}, bf16[32,256,64]{1,2,0:T(8,128)(2,1)}, u32[]{:S(2)}) copy-start(bf16[32,256,64]{1,2,0:T(8,128)(2,1)} %param.16) | copy-start | bytes 3145732
  109.0 4.4 %copy-start.3 = (f32[32,16,256]{2,1,0:T(8,128)S(1)}, f32[32,16,256]{2,1,0:T(8,128)}, u32[]{:S(2)}) copy-start(f32[32,16,256]{2,1,0:T(8,128)} %convolution_bitcast_fusion) | copy-start | bytes 1572868
